TPU v7x, 128 devices: a whole 4x4x4 slice. The times are simulated.
128 devices in a mesh: cell: 8 (over z, core), tm: 16 (over y, x).
Axes of the slice: x: 4, y: 4, z: 4, core: 2. Of those that a mesh axis runs over, the one named last changes fastest.
Arguments:
- solution: float32 [32768], P(('cell', 'tm')), may hold values from -6 to 6
- residual: float32 [32768], P(('cell', 'tm')), may hold values from -8 to 8
- direction: float32 [32768], P(('cell', 'tm')), may hold values from -8 to 8
- noise_var: float32 [32768], P(('cell', 'tm')), may hold values from 0.5 to 2
- footprints: bfloat16 [262144, 128], P(('cell', 'tm')), may hold values from -0.5 to 0.5
- tile_owner: int32 [262144, 1], P(('cell', 'tm')), may hold values from 0 to 127; in each aligned block of 2048 rows (0 to 2047, 2048 to 4095, ...) at most 32 rows name the same one
- tile_block: int32 [262144], P(('cell', 'tm')), may hold values from 0 to 8
- tile_step: int32 [262144], P(('cell', 'tm')), may hold values from 0 to 127
- tile_obs: int32 [262144], P(('cell', 'tm')), may hold values from 0 to 255
- cell_cov: bfloat16 [9216, 9216], P('cell'), may hold values from -2 to 7, as said below
- time_cov: bfloat16 [2048, 2048], P('tm'), may hold values from -2 to 7, as said below
Outputs:
- new_solution: float32 [32768], P(('cell', 'tm'))
- new_residual: float32 [32768], P(('cell', 'tm'))
- new_direction: float32 [32768], P(('cell', 'tm'))
Inputs may be any that keep to these rules, and one draw needn't show every extreme that they name: `tile_owner`: among the 2048 tiles of one device, no owner is named by more than 32 of them. `cell_cov`: symmetric positive definite. `time_cov`: symmetric positive definite.
All inputs are finite; a program needn't handle non-finite values.
Results may differ from a plain program's by a relative error of at most 0.0021.
Values may be sent and summed in bfloat16 or wider, within the bound.
A program may use at most 128 MiB of HBM per device.

v0:
```python
import functools
import jax
import jax.numpy as jnp
from jax import lax
from jax.sharding import Mesh
from jax.sharding import PartitionSpec as P

CELL = ("cell_0", "cell_1")
TM = ("tm_0", "tm_1")
CELL_TM = ("cell_0", "cell_1", "tm_0", "tm_1")


def laid_out(pieces, dim):
    lengths = list(pieces.shape[1:])
    lengths[dim] *= pieces.shape[0]
    return jnp.moveaxis(pieces, 0, dim).reshape(lengths)


def from_everyone(value, axis):
    peers = lax.axis_size(axis)
    return lax.all_to_all(
        jnp.broadcast_to(value[None], (peers, *value.shape)), axis, 0, 0, tiled=True
    )


def collect(value, axis, dim):
    return laid_out(from_everyone(value, axis), dim)


def over_axes(value, axes):
    return functools.reduce(lax.psum, axes, value)


def local(
    solution,
    residual,
    direction,
    noise_var,
    footprints,
    tile_owner,
    tile_block,
    tile_step,
    tile_obs,
    cell_cov,
    time_cov,
):
    devices = lax.axis_size(CELL) * lax.axis_size(TM)
    tile_count = footprints.shape[0]
    block_len = footprints.shape[1]
    cell_local = cell_cov.shape[0]
    time_local = time_cov.shape[0]
    block_local = cell_local // block_len
    obs_local = direction.shape[0]
    capacity = max(2, 2 * tile_count // devices)
    slot_total = devices * capacity
    owner_dev = tile_owner[:, 0]
    owner_hot = (owner_dev[:, None] == jnp.arange(devices, dtype=jnp.int32)[None, :]).astype(
        jnp.int32
    )
    slot_rank = jnp.sum(jnp.cumsum(owner_hot, axis=0) * owner_hot, axis=1) - 1
    slot_index = owner_dev * capacity + slot_rank
    obs_hot = (tile_obs[:, None] == jnp.arange(obs_local, dtype=jnp.int32)[None, :]).astype(
        jnp.float32
    )
    dir_tile = jnp.dot(obs_hot, direction, precision=lax.Precision.HIGHEST).astype(jnp.bfloat16)
    tile_place = tile_step * block_local + tile_block
    send_values = jnp.zeros((slot_total, block_len), jnp.bfloat16).at[slot_index].set(footprints)
    send_dir = jnp.zeros((slot_total,), jnp.bfloat16).at[slot_index].set(dir_tile)
    send_place = jnp.zeros((slot_total,), jnp.int32).at[slot_index].set(tile_place)
    got_values, got_dir, got_place = (
        lax.all_to_all(
            send_values.reshape(devices, capacity, block_len),
            CELL_TM,
            split_axis=0,
            concat_axis=0,
            tiled=True,
        ),
        lax.all_to_all(
            send_dir.reshape(devices, capacity), CELL_TM, split_axis=0, concat_axis=0, tiled=True
        ),
        lax.all_to_all(
            send_place.reshape(devices, capacity), CELL_TM, split_axis=0, concat_axis=0, tiled=True
        ),
    )
    got_values = got_values.reshape(slot_total, block_len).astype(jnp.float32)
    got_dir = got_dir.reshape(slot_total).astype(jnp.float32)
    got_place = got_place.reshape(slot_total)
    flux_time = jnp.zeros((time_local * block_local, block_len), jnp.float32)
    flux_time = flux_time.at[got_place].add(got_dir[:, None] * got_values)
    flux_grid = flux_time.reshape(time_local, cell_local).T.astype(jnp.bfloat16)
    mixed_cells = jnp.dot(
        cell_cov, collect(flux_grid, CELL, 0), preferred_element_type=jnp.float32
    ).astype(jnp.bfloat16)
    smoothed = lax.dot_general(
        time_cov,
        lax.all_gather(mixed_cells, TM, axis=1, tiled=True),
        (((1,), (1,)), ((), ())),
        preferred_element_type=jnp.float32,
    )
    smoothed = smoothed.astype(jnp.bfloat16).reshape(time_local * block_local, block_len)
    slot_dots = jnp.sum(got_values * smoothed[got_place].astype(jnp.float32), axis=1)
    returned = lax.all_to_all(
        slot_dots.reshape(devices, capacity), CELL_TM, split_axis=0, concat_axis=0, tiled=True
    )
    tile_dots = returned.reshape(slot_total)[slot_index]
    applied = jnp.dot(tile_dots, obs_hot, precision=lax.Precision.HIGHEST) + noise_var * direction
    norm_now, curvature, cross_term, image_norm = (
        over_axes(jnp.sum(residual * residual), CELL_TM),
        over_axes(jnp.sum(direction * applied), CELL_TM),
        over_axes(jnp.sum(residual * applied), CELL_TM),
        over_axes(jnp.sum(applied * applied), CELL_TM),
    )
    step_size = norm_now / curvature
    new_solution = solution + step_size * direction
    new_residual = residual - step_size * applied
    norm_next = norm_now - 2.0 * step_size * cross_term + step_size * step_size * image_norm
    new_direction = new_residual + norm_next / norm_now * direction
    return (new_solution, new_residual, new_direction)


def solution(mesh):
    finer = Mesh(mesh.devices.reshape(4, 2, 4, 4), ("cell_0", "cell_1", "tm_0", "tm_1"))
    in_specs = (
        P(CELL_TM),
        P(CELL_TM),
        P(CELL_TM),
        P(CELL_TM),
        P(CELL_TM, None),
        P(CELL_TM, None),
        P(CELL_TM),
        P(CELL_TM),
        P(CELL_TM),
        P(CELL, None),
        P(TM, None),
    )
    out_specs = (P(CELL_TM), P(CELL_TM), P(CELL_TM))
    return jax.shard_map(local, mesh=finer, in_specs=in_specs, out_specs=out_specs, check_vma=False)
```

profile of v0, /device:TPU:0, one launch (start us, length us, event | category | flops | bytes accessed | tf_op | source)
XLA Modules:
  0.0 305.8 jit_solution(9273110876222847107)
XLA Ops:
  7.2 0.9 copy.20
  8.0 0.3 fusion.8
  8.6 0.3 copy.21
  8.9 0.2 copy-done.1
  9.1 0.6 fusion.5
  9.8 1.0 fusion.4
  10.9 14.6 %scatter_custom_fusion.2 = bf16[4096]{0:T(1024)(128)(2,1)S(1)} fusion(s32[2048]{0:T(1024)S(1)} %bitcast.43, bf16[2048]{0:T(1024)(128)(2,1)S(1)} %convert_element_type.58, bf16[]{:T(256)} %constant.10.clone.1), kind=kCustom, calls=%fused_computation.39 | custom fusion | bytes 8194 | tf_op jit(solution)/shard_map/scatter | solution.py:68
  25.5 0.7 all_to_all.32
  26.2 11.2 %all-to-all-start.2 = ((bf16[128,1,32]{2,1,0:T(2,128)(2,1)}), bf16[128,1,32]{2,1,0:T(2,128)(2,1)S(1)}, u32[]{:S(2)}, u32[]{:S(2)}) async-start(bf16[128,1,32]{2,1,0:T(2,128)(2,1)} %all_to_all.32), calls=%async_computation.2 | async-start | bytes 131072 | tf_op jit(solution)/shard_map/all_to_all | solution.py:78
  37.4 8.1 %scatter_custom_fusion.1 = s32[4096]{0:T(1024)S(1)} fusion(s32[2048]{0:T(1024)S(1)} %bitcast.44, s32[2048]{0:T(1024)S(1)} %multiply_add_fusion, s32[]{:T(128)} %constant.12.clone.1), kind=kCustom, calls=%fused_computation.36 | custom fusion | bytes 16388 | tf_op jit(solution)/shard_map/scatter | solution.py:69
  45.5 0.7 all_to_all.25
  46.2 0.7 all-to-all-done.2
  46.9 9.1 %all-to-all-start.1 = ((s32[128,1,32]{2,1,0:T(1,128)}), s32[128,1,32]{2,1,0:T(1,128)S(1)}, u32[]{:S(2)}, u32[]{:S(2)}) async-start(s32[128,1,32]{2,1,0:T(1,128)} %bitcast.8), calls=%async_computation.1 | async-start | bytes 131072 | tf_op jit(solution)/shard_map/all_to_all | solution.py:81
  55.9 7.2 %scatter_custom_fusion = bf16[4096,128]{1,0:T(8,128)(2,1)} fusion(s32[2048]{0:T(1024)S(1)} %bitcast.45, bf16[2048,128]{1,0:T(8,128)(2,1)} %param.15, bf16[]{:T(256)} %constant.10.clone.1), kind=kCustom, calls=%fused_computation.26 | custom fusion | bytes 1049088 | tf_op jit(solution)/shard_map/scatter | solution.py:67
  63.1 2.3 all-to-all-done.1
  65.4 7.4 %all-to-all-start = ((bf16[128,32,128]{2,1,0:T(8,128)(2,1)}), bf16[128,32,128]{2,1,0:T(8,128)(2,1)S(1)}, u32[]{:S(2)}, u32[]{:S(2)}) async-start(bf16[128,32,128]{2,1,0:T(8,128)(2,1)} %bitcast.7), calls=%async_computation | async-start | bytes 2097152 | tf_op jit(solution)/shard_map/all_to_all | solution.py:71
  72.9 0.2 all-gather.2.cloned.1.call-start
  73.1 0.2 convert_reduce_fusion
  73.3 0.1 reshape.115
  73.4 0.5 broadcast.93
  73.9 0.8 reduce.11
  74.7 0.1 reshape.111
  74.8 17.1 %all-to-all-done = bf16[128,32,128]{2,1,0:T(8,128)(2,1)S(1)} async-done(((bf16[128,32,128]{2,1,0:T(8,128)(2,1)}), bf16[128,32,128]{2,1,0:T(8,128)(2,1)S(1)}, u32[]{:S(2)}, u32[]{:S(2)}) %all-to-all-start) | async-done | bytes 1048608 | tf_op jit(solution)/shard_map/all_to_all | solution.py:71
  91.9 2.0 bitcast_multiply_fusion
  93.9 23.6 %scatter_custom_fusion.3 = f32[1152,128]{1,0:T(8,128)S(1)} fusion(s32[4096]{0:T(1024)S(1)} %bitcast.41, f32[4096,128]{1,0:T(8,128)} %bitcast_multiply_fusion, f32[]{:T(128)} %constant.9.clone.1), kind=kCustom, calls=%fused_computation.28 | custom fusion | flops 524288 | bytes 590336 | tf_op jit(solution)/shard_map/scatter-add | solution.py:89
  117.5 0.4 convert_element_type.64
  117.9 0.2 copy.24
  118.1 0.3 broadcast_in_dim.11
  118.4 33.0 %all_to_all.38 = bf16[8,1152,128]{2,1,0:T(8,128)(2,1)S(1)} all-to-all(bf16[8,1152,128]{2,1,0:T(8,128)(2,1)S(1)} %broadcast_in_dim.11), channel_id=1, replica_groups=mesh['cell_0'=4,'cell_1'=2,'tm_0'=4,'tm_1'=4] {'cell_0','cell_1'}, dimensions={0} | all-to-all | bytes 4718592 | tf_op jit(solution)/shard_map/all_to_all | solution.py:21
  151.4 11.7 %fusion.1 = bf16[1152,128]{0,1:T(8,128)(2,1)} fusion(bf16[9216,128]{1,0:T(8,128)(2,1)S(1)} %bitcast.36, bf16[1152,9216]{1,0:T(8,128)(2,1)} %param.20), kind=kOutput, calls=%fused_computation.9 | convolution fusion | flops 2718056448 | bytes 23887872 | tf_op jit(solution)/shard_map/dot_general | solution.py:91
  163.1 49.9 %all-gather.2.cloned.1.call-done = bf16[1152,2048]{0,1:T(8,128)(2,1)} async-done(((bf16[1152,128]{0,1:T(8,128)(2,1)}), bf16[1152,2048]{0,1:T(8,128)(2,1)}) %all-gather.2.cloned.1.call-update) | async-done | bytes 4718608 | tf_op jit(solution)/shard_map/all_gather | solution.py:96
  213.0 3.8 %fusion = bf16[128,1152]{0,1:T(8,128)(2,1)S(1)} fusion(bf16[1152,2048]{0,1:T(8,128)(2,1)} %all-gather.2.cloned.1.call-done, bf16[128,2048]{1,0:T(8,128)(2,1)S(1)} %copy-done), kind=kOutput, calls=%fused_computation.8 | convolution fusion | flops 604127232 | bytes 5537792 | tf_op jit(solution)/shard_map/dot_general | solution.py:94
  216.8 0.2 copy.25
  217.0 0.3 reshape.113
  217.4 12.1 %gather_fusion = bf16[4096,128]{1,0:T(8,128)(2,1)S(1)} fusion(bf16[1152,128]{1,0:T(8,128)(2,1)S(1)} %reshape.113, s32[4096]{0:T(1024)S(1)} %broadcast_clamp_fusion), kind=kCustom, calls=%fused_computation | custom fusion | bytes 2113536 | tf_op jit(solution)/shard_map/gather | solution.py:101
  229.5 1.3 fusion.2
  230.8 8.4 %all-to-all-start.4 = ((f32[128,1,32]{2,1,0:T(1,128)}), f32[128,1,32]{2,1,0:T(1,128)S(1)}, u32[]{:S(2)}, u32[]{:S(2)}) async-start(f32[128,1,32]{2,1,0:T(1,128)} %bitcast.18), calls=%async_computation.4 | async-start | bytes 131072 | tf_op jit(solution)/shard_map/all_to_all | solution.py:102
  239.2 9.5 %all-to-all-done.4 = f32[128,1,32]{2,1,0:T(1,128)S(1)} async-done(((f32[128,1,32]{2,1,0:T(1,128)}), f32[128,1,32]{2,1,0:T(1,128)S(1)}, u32[]{:S(2)}, u32[]{:S(2)}) %all-to-all-start.4) | async-done | bytes 16416 | tf_op jit(solution)/shard_map/all_to_all | solution.py:102
  248.7 0.5 broadcast.94
  249.2 0.8 reduce.12
  250.1 11.8 %gather_fusion.1 = f32[2048]{0:T(1024)S(1)} fusion(f32[4096]{0:T(1024)S(1)} %reshape.114, s32[2048]{0:T(1024)S(1)} %broadcast_clamp_fusion.1), kind=kCustom, calls=%fused_computation.1 | custom fusion | bytes 24576 | tf_op jit(solution)/shard_map/gather | solution.py:105
  261.9 0.8 fusion.3
  262.7 0.6 multiply_reduce_fusion
  263.3 9.3 %all-reduce.2 = (f32[]{:T(128)}, f32[]{:T(128)}, f32[]{:T(128)}, f32[]{:T(128)}) all-reduce(f32[]{:T(128)} %get-tuple-element.5, f32[]{:T(128)} %get-tuple-element.6, f32[]{:T(128)} %get-tuple-element.4, f32[]{:T(128)} %get-tuple-element.3), channel_id=1, replica_groups=mesh['cell_0'=4,'cell_1'=2,'tm_0'=4,'tm_1'=4] {'cell_0'}, use_global_device_ids=true, to_apply=%region_1.2 | all-reduce | flops 4 | bytes 32 | tf_op jit(solution)/shard_map/psum | solution.py:31
  272.6 3.1 %all-reduce.3 = (f32[]{:T(128)}, f32[]{:T(128)}, f32[]{:T(128)}, f32[]{:T(128)}) all-reduce(f32[]{:T(128)} %get-tuple-element.15, f32[]{:T(128)} %get-tuple-element.16, f32[]{:T(128)} %get-tuple-element.17, f32[]{:T(128)} %get-tuple-element.18), channel_id=1, replica_groups=mesh['cell_0'=4,'cell_1'=2,'tm_0'=4,'tm_1'=4] {'cell_1'}, use_global_device_ids=true, to_apply=%region_2.3 | all-reduce | flops 4 | bytes 32 | tf_op jit(solution)/shard_map/psum | solution.py:31
  275.7 9.1 %all-reduce.1 = (f32[]{:T(128)}, f32[]{:T(128)}, f32[]{:T(128)}, f32[]{:T(128)}) all-reduce(f32[]{:T(128)} %get-tuple-element.19, f32[]{:T(128)} %get-tuple-element.20, f32[]{:T(128)} %get-tuple-element.21, f32[]{:T(128)} %get-tuple-element.22), channel_id=1, replica_groups=mesh['cell_0'=4,'cell_1'=2,'tm_0'=4,'tm_1'=4] {'tm_0'}, use_global_device_ids=true, to_apply=%region_3.4 | all-reduce | flops 4 | bytes 32 | tf_op jit(solution)/shard_map/psum | solution.py:31
  284.8 9.7 %all-reduce = (f32[]{:T(128)}, f32[]{:T(128)}, f32[]{:T(128)}, f32[]{:T(128)}) all-reduce(f32[]{:T(128)} %get-tuple-element.11, f32[]{:T(128)} %get-tuple-element.12, f32[]{:T(128)} %get-tuple-element.13, f32[]{:T(128)} %get-tuple-element.14), channel_id=1, replica_groups=mesh['cell_0'=4,'cell_1'=2,'tm_0'=4,'tm_1'=4] {'tm_1'}, use_global_device_ids=true, to_apply=%region_4.5 | all-reduce | flops 4 | bytes 32 | tf_op jit(solution)/shard_map/psum | solution.py:31
  298.3 0.6 multiply_add_fusion.1
  (31 shorter events, 0.4 us)
Async XLA Ops:
  7.2 205.9 %copy-start = (bf16[128,2048]{1,0:T(8,128)(2,1)S(1)}, bf16[128,2048]{1,0:T(8,128)(2,1)}, u32[]{:S(2)}) copy-start(bf16[128,2048]{1,0:T(8,128)(2,1)} %param.21) | copy-start | bytes 1572868
  8.4 0.7 copy-start.1
  8.5 1.3 copy-start.4
  8.5 1.3 copy-start.8
  8.5 28.8 %copy-start.2 = (s32[2048]{0:T(1024)S(1)}, s32[2048]{0:T(1024)}, u32[]{:S(2)}) copy-start(s32[2048]{0:T(1024)} %param.17) | copy-start | bytes 24580
  8.6 28.8 %copy-start.3 = (s32[2048]{0:T(1024)S(1)}, s32[2048]{0:T(1024)}, u32[]{:S(2)}) copy-start(s32[2048]{0:T(1024)} %param.18) | copy-start | bytes 24580
  26.2 20.7 %all-to-all-start.2 = ((bf16[128,1,32]{2,1,0:T(2,128)(2,1)}), bf16[128,1,32]{2,1,0:T(2,128)(2,1)S(1)}, u32[]{:S(2)}, u32[]{:S(2)}) async-start(bf16[128,1,32]{2,1,0:T(2,128)(2,1)} %all_to_all.32), calls=%async_computation.2 | async-start | bytes 131072 | tf_op jit(solution)/shard_map/all_to_all | solution.py:78
  46.9 18.6 %all-to-all-start.1 = ((s32[128,1,32]{2,1,0:T(1,128)}), s32[128,1,32]{2,1,0:T(1,128)S(1)}, u32[]{:S(2)}, u32[]{:S(2)}) async-start(s32[128,1,32]{2,1,0:T(1,128)} %bitcast.8), calls=%async_computation.1 | async-start | bytes 131072 | tf_op jit(solution)/shard_map/all_to_all | solution.py:81
  65.4 26.5 %all-to-all-start = ((bf16[128,32,128]{2,1,0:T(8,128)(2,1)}), bf16[128,32,128]{2,1,0:T(8,128)(2,1)S(1)}, u32[]{:S(2)}, u32[]{:S(2)}) async-start(bf16[128,32,128]{2,1,0:T(8,128)(2,1)} %bitcast.7), calls=%async_computation | async-start | bytes 2097152 | tf_op jit(solution)/shard_map/all_to_all | solution.py:71
  72.9 140.2 %all-gather.2.cloned.1.call-start = ((), (), s32[]{:S(2)}) async-start(), calls=%async_computation.5 | async-start | bytes 5013504 | tf_op jit(solution)/shard_map/all_gather | solution.py:96
  230.8 17.9 %all-to-all-start.4 = ((f32[128,1,32]{2,1,0:T(1,128)}), f32[128,1,32]{2,1,0:T(1,128)S(1)}, u32[]{:S(2)}, u32[]{:S(2)}) async-start(f32[128,1,32]{2,1,0:T(1,128)} %bitcast.18), calls=%async_computation.4 | async-start | bytes 131072 | tf_op jit(solution)/shard_map/all_to_all | solution.py:102
  250.1 12.6 %copy-start.5 = (f32[256]{0:T(256)S(1)}, f32[256]{0:T(256)}, u32[]{:S(2)}) copy-start(f32[256]{0:T(256)} %param.12) | copy-start | bytes 3076
  250.1 12.6 %copy-start.6 = (f32[256]{0:T(256)S(1)}, f32[256]{0:T(256)}, u32[]{:S(2)}) copy-start(f32[256]{0:T(256)} %param.14) | copy-start | bytes 3076
  250.1 48.3 %copy-start.7 = (f32[256]{0:T(256)S(1)}, f32[256]{0:T(256)}, u32[]{:S(2)}) copy-start(f32[256]{0:T(256)} %param.11) | copy-start | bytes 3076
Sparse Core Ops, SparseCore 0:
  163.2 49.7 all-gather.1
where the time goes:
time: 306 us
  waiting for transfers between devices  79.5 us (26%)
  blocking collectives  64.2 us (21%)
  local copies, waits for them, and re-layouts  59.3 us (19%)
  starting transfers between devices  36.3 us (12%)
  other arithmetic  31 us (10%)
  between operations  18.3 us (6%)
  matrix products  17.3 us (6%)
    all_gather x1, waiting for transfers between devices, local(): lax.all_gather(mixed_cells, TM, axis=1, tiled=True)  49.9 us
    all_to_all x1, blocking collectives, from_everyone(): lax.all_to_all(jnp.broadcast_to(value[None], (peers, *value.shape)), axis...  33 us
    psum x4, blocking collectives, over_axes(): return functools.reduce(lax.psum, axes, value)  31.2 us
    scatter-add x1, other arithmetic, local(): flux_time = flux_time.at[got_place].add(got_dir[:, None] * got_values)  23.6 us
    all_to_all x1, waiting for transfers between devices, local(): lax.all_to_all(send_values.reshape(devices, capacity, block_len), CELL_TM...  17.1 us
    scatter x1, local copies, waits for them, and re-layouts, local(): jnp.zeros((slot_total,), jnp.bfloat16).at[slot_index].set(dir_tile)  14.6 us
    gather x1, local copies, waits for them, and re-layouts, local(): smoothed[got_place].astype(jnp.float32)  12.1 us
    gather x1, local copies, waits for them, and re-layouts, local(): tile_dots = returned.reshape(slot_total)[slot_index]  11.8 us
  transfers between devices with their start and end apart: 5, of which 5 were waited for; matrix products, arithmetic and copies ran while one was open for 6% of the time, Pallas kernels for 0%

commit v1 on v0

--- a/solution.py
+++ b/solution.py
@@ -93,7 +93,9 @@
     ).astype(jnp.bfloat16)
     smoothed = lax.dot_general(
         time_cov,
-        lax.all_gather(mixed_cells, TM, axis=1, tiled=True),
+        jnp.concatenate(
+            lax.all_to_all(jnp.stack([mixed_cells] * lax.axis_size(TM)), TM, 0, 0), axis=1
+        ),
         (((1,), (1,)), ((), ())),
         preferred_element_type=jnp.float32,
     )

time: 306 us -> 319 us (1.042)
  waiting for transfers between devices: 79.5 us -> 100 us
  between operations: 18.3 us -> 4.88 us
    all_to_all x0 -> x1, waiting for transfers between devices: none -> 70.6 us  [local(): lax.all_to_all(jnp.stack([mixed_cells] * lax.axis_size(TM)), TM, 0, 0)]
    all_gather x1 -> x0, waiting for transfers between devices: 49.9 us -> none  [local(): lax.all_gather(mixed_cells, TM, axis=1, tiled=True)]
    all_to_all x0 -> x1, starting transfers between devices: none -> 4.56 us  [local(): lax.all_to_all(jnp.stack([mixed_cells] * lax.axis_size(TM)), TM, 0, 0)]
  transfers between devices with their start and end apart: 5 -> 5, of which waited for: 5 -> 5; matrix products, arithmetic and copies ran while one was open for 6% -> 5% of each run, Pallas kernels for 0% -> 0%
where the time goes in v1:
time: 319 us; the launch traced here: 318 us
  waiting for transfers between devices  100 us (31%)
  blocking collectives  64.2 us (20%)
  local copies, waits for them, and re-layouts  62.1 us (19%)
  starting transfers between devices  38.9 us (12%)
  other arithmetic  30.9 us (10%)
  matrix products  16.8 us (5%)
  between operations  4.88 us (2%)
    all_to_all x1, waiting for transfers between devices, local(): lax.all_to_all(jnp.stack([mixed_cells] * lax.axis_size(TM)), TM, 0, 0)  70.6 us
    all_to_all x1, blocking collectives, from_everyone(): lax.all_to_all(jnp.broadcast_to(value[None], (peers, *value.shape)), axis...  33 us
    psum x4, blocking collectives, over_axes(): return functools.reduce(lax.psum, axes, value)  31.2 us
    scatter-add x1, other arithmetic, local(): flux_time = flux_time.at[got_place].add(got_dir[:, None] * got_values)  23.6 us
    all_to_all x1, waiting for transfers between devices, local(): lax.all_to_all(send_values.reshape(devices, capacity, block_len), CELL_TM...  17.1 us
    scatter x1, local copies, waits for them, and re-layouts, local(): jnp.zeros((slot_total,), jnp.bfloat16).at[slot_index].set(dir_tile)  14.6 us
    gather x1, local copies, waits for them, and re-layouts, local(): smoothed[got_place].astype(jnp.float32)  12.1 us
    gather x1, local copies, waits for them, and re-layouts, local(): tile_dots = returned.reshape(slot_total)[slot_index]  11.8 us
  transfers between devices with their start and end apart: 5, of which 5 were waited for; matrix products, arithmetic and copies ran while one was open for 5% of the time, Pallas kernels for 0%

profile of v1, /device:TPU:0, one launch (start us, length us, event | category | flops | bytes accessed | tf_op | source)
XLA Modules:
  0.0 318.0 jit_solution(14926898839526370508)
XLA Ops:
  0.6 0.9 copy.21
  1.5 0.3 fusion.8
  2.0 0.3 copy.22
  2.4 0.2 copy-done.1
  2.6 0.6 fusion.5
  3.3 1.0 fusion.4
  4.3 14.6 %scatter_custom_fusion.2 = bf16[4096]{0:T(1024)(128)(2,1)S(1)} fusion(s32[2048]{0:T(1024)S(1)} %bitcast.46, bf16[2048]{0:T(1024)(128)(2,1)S(1)} %convert_element_type.58, bf16[]{:T(256)} %constant.10.clone.1), kind=kCustom, calls=%fused_computation.39 | custom fusion | bytes 8194 | tf_op jit(solution)/shard_map/scatter | solution.py:68
  18.9 0.7 all_to_all.36
  19.6 11.2 %all-to-all-start.2 = ((bf16[128,1,32]{2,1,0:T(2,128)(2,1)}), bf16[128,1,32]{2,1,0:T(2,128)(2,1)S(1)}, u32[]{:S(2)}, u32[]{:S(2)}) async-start(bf16[128,1,32]{2,1,0:T(2,128)(2,1)} %all_to_all.36), calls=%async_computation.2 | async-start | bytes 131072 | tf_op jit(solution)/shard_map/all_to_all | solution.py:78
  30.9 8.1 %scatter_custom_fusion.1 = s32[4096]{0:T(1024)S(1)} fusion(s32[2048]{0:T(1024)S(1)} %bitcast.47, s32[2048]{0:T(1024)S(1)} %multiply_add_fusion, s32[]{:T(128)} %constant.12.clone.1), kind=kCustom, calls=%fused_computation.36 | custom fusion | bytes 16388 | tf_op jit(solution)/shard_map/scatter | solution.py:69
  38.9 0.7 all_to_all.28
  39.6 0.7 all-to-all-done.2
  40.3 9.1 %all-to-all-start.1 = ((s32[128,1,32]{2,1,0:T(1,128)}), s32[128,1,32]{2,1,0:T(1,128)S(1)}, u32[]{:S(2)}, u32[]{:S(2)}) async-start(s32[128,1,32]{2,1,0:T(1,128)} %bitcast.8), calls=%async_computation.1 | async-start | bytes 131072 | tf_op jit(solution)/shard_map/all_to_all | solution.py:81
  49.4 7.2 %scatter_custom_fusion = bf16[4096,128]{1,0:T(8,128)(2,1)} fusion(s32[2048]{0:T(1024)S(1)} %bitcast.48, bf16[2048,128]{1,0:T(8,128)(2,1)} %param.15, bf16[]{:T(256)} %constant.10.clone.1), kind=kCustom, calls=%fused_computation.26 | custom fusion | bytes 1049088 | tf_op jit(solution)/shard_map/scatter | solution.py:67
  56.6 2.3 all-to-all-done.1
  58.9 7.6 %all-to-all-start = ((bf16[128,32,128]{2,1,0:T(8,128)(2,1)}), bf16[128,32,128]{2,1,0:T(8,128)(2,1)S(1)}, u32[]{:S(2)}, u32[]{:S(2)}) async-start(bf16[128,32,128]{2,1,0:T(8,128)(2,1)} %bitcast.7), calls=%async_computation | async-start | bytes 2097152 | tf_op jit(solution)/shard_map/all_to_all | solution.py:71
  66.5 0.2 convert_reduce_fusion
  66.8 0.5 broadcast.95
  67.3 0.8 reduce.11
  68.1 0.1 reshape.119
  68.2 17.1 %all-to-all-done = bf16[128,32,128]{2,1,0:T(8,128)(2,1)S(1)} async-done(((bf16[128,32,128]{2,1,0:T(8,128)(2,1)}), bf16[128,32,128]{2,1,0:T(8,128)(2,1)S(1)}, u32[]{:S(2)}, u32[]{:S(2)}) %all-to-all-start) | async-done | bytes 1048608 | tf_op jit(solution)/shard_map/all_to_all | solution.py:71
  85.4 2.0 bitcast_multiply_fusion
  87.3 23.6 %scatter_custom_fusion.3 = f32[1152,128]{1,0:T(8,128)S(1)} fusion(s32[4096]{0:T(1024)S(1)} %bitcast.44, f32[4096,128]{1,0:T(8,128)} %bitcast_multiply_fusion, f32[]{:T(128)} %constant.9.clone.1), kind=kCustom, calls=%fused_computation.28 | custom fusion | flops 524288 | bytes 590336 | tf_op jit(solution)/shard_map/scatter-add | solution.py:89
  110.9 0.4 convert_element_type.64
  111.3 0.2 copy.25
  111.5 0.3 broadcast_in_dim.11
  111.8 33.0 %all_to_all.43 = bf16[8,1152,128]{2,1,0:T(8,128)(2,1)S(1)} all-to-all(bf16[8,1152,128]{2,1,0:T(8,128)(2,1)S(1)} %broadcast_in_dim.11), channel_id=1, replica_groups=mesh['cell_0'=4,'cell_1'=2,'tm_0'=4,'tm_1'=4] {'cell_0','cell_1'}, dimensions={0} | all-to-all | bytes 4718592 | tf_op jit(solution)/shard_map/all_to_all | solution.py:21
  144.9 11.2 %fusion.1 = bf16[1152,128]{0,1:T(8,128)(2,1)S(1)} fusion(bf16[9216,128]{1,0:T(8,128)(2,1)S(1)} %bitcast.39, bf16[1152,9216]{1,0:T(8,128)(2,1)} %param.20), kind=kOutput, calls=%fused_computation.9 | convolution fusion | flops 2718056448 | bytes 23887872 | tf_op jit(solution)/shard_map/dot_general | solution.py:91
  156.0 2.8 stack.2
  158.8 4.6 %all-to-all-start.4 = ((bf16[16,1152,128]{1,2,0:T(8,128)(2,1)}), bf16[16,1152,128]{1,2,0:T(8,128)(2,1)}, u32[]{:S(2)}, u32[]{:S(2)}) async-start(bf16[16,1152,128]{1,2,0:T(8,128)(2,1)} %stack.2), calls=%async_computation.4 | async-start | bytes 9437184 | tf_op jit(solution)/shard_map/all_to_all | solution.py:97
  163.4 70.6 %all-to-all-done.4 = bf16[16,1152,128]{1,2,0:T(8,128)(2,1)} async-done(((bf16[16,1152,128]{1,2,0:T(8,128)(2,1)}), bf16[16,1152,128]{1,2,0:T(8,128)(2,1)}, u32[]{:S(2)}, u32[]{:S(2)}) %all-to-all-start.4) | async-done | bytes 4718624 | tf_op jit(solution)/shard_map/all_to_all | solution.py:97
  234.0 3.8 %fusion = bf16[128,1152]{0,1:T(8,128)(2,1)S(1)} fusion(bf16[1152,2048]{0,1:T(8,128)(2,1)} %bitcast.17, bf16[128,2048]{1,0:T(8,128)(2,1)S(1)} %copy-done), kind=kOutput, calls=%fused_computation.8 | convolution fusion | flops 604127232 | bytes 5537792 | tf_op jit(solution)/shard_map/dot_general | solution.py:94
  237.8 0.2 copy.26
  238.0 0.3 reshape.123
  238.3 12.1 %gather_fusion = bf16[4096,128]{1,0:T(8,128)(2,1)S(1)} fusion(bf16[1152,128]{1,0:T(8,128)(2,1)S(1)} %reshape.123, s32[4096]{0:T(1024)S(1)} %broadcast_clamp_fusion), kind=kCustom, calls=%fused_computation | custom fusion | bytes 2113536 | tf_op jit(solution)/shard_map/gather | solution.py:103
  250.5 1.2 fusion.2
  251.7 6.5 %all-to-all-start.5 = ((f32[128,1,32]{2,1,0:T(1,128)}), f32[128,1,32]{2,1,0:T(1,128)S(1)}, u32[]{:S(2)}, u32[]{:S(2)}) async-start(f32[128,1,32]{2,1,0:T(1,128)} %bitcast.20), calls=%async_computation.5 | async-start | bytes 131072 | tf_op jit(solution)/shard_map/all_to_all | solution.py:104
  258.2 9.5 %all-to-all-done.5 = f32[128,1,32]{2,1,0:T(1,128)S(1)} async-done(((f32[128,1,32]{2,1,0:T(1,128)}), f32[128,1,32]{2,1,0:T(1,128)S(1)}, u32[]{:S(2)}, u32[]{:S(2)}) %all-to-all-start.5) | async-done | bytes 16416 | tf_op jit(solution)/shard_map/all_to_all | solution.py:104
  267.7 0.5 broadcast.96
  268.2 0.8 reduce.12
  269.2 11.8 %gather_fusion.1 = f32[2048]{0:T(1024)S(1)} fusion(f32[4096]{0:T(1024)S(1)} %reshape.124, s32[2048]{0:T(1024)S(1)} %broadcast_clamp_fusion.1), kind=kCustom, calls=%fused_computation.1 | custom fusion | bytes 24576 | tf_op jit(solution)/shard_map/gather | solution.py:107
  281.0 0.8 fusion.3
  281.8 0.6 multiply_reduce_fusion
  282.4 9.3 %all-reduce.2 = (f32[]{:T(128)}, f32[]{:T(128)}, f32[]{:T(128)}, f32[]{:T(128)}) all-reduce(f32[]{:T(128)} %get-tuple-element.5, f32[]{:T(128)} %get-tuple-element.6, f32[]{:T(128)} %get-tuple-element.4, f32[]{:T(128)} %get-tuple-element.3), channel_id=1, replica_groups=mesh['cell_0'=4,'cell_1'=2,'tm_0'=4,'tm_1'=4] {'cell_0'}, use_global_device_ids=true, to_apply=%region_1.2 | all-reduce | flops 4 | bytes 32 | tf_op jit(solution)/shard_map/psum | solution.py:31
  291.7 3.1 all-reduce.3
  294.8 9.1 %all-reduce.1 = (f32[]{:T(128)}, f32[]{:T(128)}, f32[]{:T(128)}, f32[]{:T(128)}) all-reduce(f32[]{:T(128)} %get-tuple-element.19, f32[]{:T(128)} %get-tuple-element.20, f32[]{:T(128)} %get-tuple-element.21, f32[]{:T(128)} %get-tuple-element.22), channel_id=1, replica_groups=mesh['cell_0'=4,'cell_1'=2,'tm_0'=4,'tm_1'=4] {'tm_0'}, use_global_device_ids=true, to_apply=%region_3.4 | all-reduce | flops 4 | bytes 32 | tf_op jit(solution)/shard_map/psum | solution.py:31
  303.9 9.7 %all-reduce = (f32[]{:T(128)}, f32[]{:T(128)}, f32[]{:T(128)}, f32[]{:T(128)}) all-reduce(f32[]{:T(128)} %get-tuple-element.11, f32[]{:T(128)} %get-tuple-element.12, f32[]{:T(128)} %get-tuple-element.13, f32[]{:T(128)} %get-tuple-element.14), channel_id=1, replica_groups=mesh['cell_0'=4,'cell_1'=2,'tm_0'=4,'tm_1'=4] {'tm_1'}, use_global_device_ids=true, to_apply=%region_4.5 | all-reduce | flops 4 | bytes 32 | tf_op jit(solution)/shard_map/psum | solution.py:31
  317.4 0.6 multiply_add_fusion.1
  (31 shorter events, 0.4 us)
Async XLA Ops:
  0.6 233.4 %copy-start = (bf16[128,2048]{1,0:T(8,128)(2,1)S(1)}, bf16[128,2048]{1,0:T(8,128)(2,1)}, u32[]{:S(2)}) copy-start(bf16[128,2048]{1,0:T(8,128)(2,1)} %param.21) | copy-start | bytes 1572868
  1.9 0.7 copy-start.1
  2.0 1.3 copy-start.4
  2.0 1.3 copy-start.8
  2.0 28.8 %copy-start.2 = (s32[2048]{0:T(1024)S(1)}, s32[2048]{0:T(1024)}, u32[]{:S(2)}) copy-start(s32[2048]{0:T(1024)} %param.17) | copy-start | bytes 24580
  2.0 28.8 %copy-start.3 = (s32[2048]{0:T(1024)S(1)}, s32[2048]{0:T(1024)}, u32[]{:S(2)}) copy-start(s32[2048]{0:T(1024)} %param.18) | copy-start | bytes 24580
  19.6 20.7 %all-to-all-start.2 = ((bf16[128,1,32]{2,1,0:T(2,128)(2,1)}), bf16[128,1,32]{2,1,0:T(2,128)(2,1)S(1)}, u32[]{:S(2)}, u32[]{:S(2)}) async-start(bf16[128,1,32]{2,1,0:T(2,128)(2,1)} %all_to_all.36), calls=%async_computation.2 | async-start | bytes 131072 | tf_op jit(solution)/shard_map/all_to_all | solution.py:78
  40.3 18.6 %all-to-all-start.1 = ((s32[128,1,32]{2,1,0:T(1,128)}), s32[128,1,32]{2,1,0:T(1,128)S(1)}, u32[]{:S(2)}, u32[]{:S(2)}) async-start(s32[128,1,32]{2,1,0:T(1,128)} %bitcast.8), calls=%async_computation.1 | async-start | bytes 131072 | tf_op jit(solution)/shard_map/all_to_all | solution.py:81
  58.9 26.5 %all-to-all-start = ((bf16[128,32,128]{2,1,0:T(8,128)(2,1)}), bf16[128,32,128]{2,1,0:T(8,128)(2,1)S(1)}, u32[]{:S(2)}, u32[]{:S(2)}) async-start(bf16[128,32,128]{2,1,0:T(8,128)(2,1)} %bitcast.7), calls=%async_computation | async-start | bytes 2097152 | tf_op jit(solution)/shard_map/all_to_all | solution.py:71
  158.8 75.2 %all-to-all-start.4 = ((bf16[16,1152,128]{1,2,0:T(8,128)(2,1)}), bf16[16,1152,128]{1,2,0:T(8,128)(2,1)}, u32[]{:S(2)}, u32[]{:S(2)}) async-start(bf16[16,1152,128]{1,2,0:T(8,128)(2,1)} %stack.2), calls=%async_computation.4 | async-start | bytes 9437184 | tf_op jit(solution)/shard_map/all_to_all | solution.py:97
  251.7 16.0 %all-to-all-start.5 = ((f32[128,1,32]{2,1,0:T(1,128)}), f32[128,1,32]{2,1,0:T(1,128)S(1)}, u32[]{:S(2)}, u32[]{:S(2)}) async-start(f32[128,1,32]{2,1,0:T(1,128)} %bitcast.20), calls=%async_computation.5 | async-start | bytes 131072 | tf_op jit(solution)/shard_map/all_to_all | solution.py:104
  269.1 12.6 %copy-start.5 = (f32[256]{0:T(256)S(1)}, f32[256]{0:T(256)}, u32[]{:S(2)}) copy-start(f32[256]{0:T(256)} %param.12) | copy-start | bytes 3076
  269.1 12.6 %copy-start.6 = (f32[256]{0:T(256)S(1)}, f32[256]{0:T(256)}, u32[]{:S(2)}) copy-start(f32[256]{0:T(256)} %param.14) | copy-start | bytes 3076
  269.2 48.3 %copy-start.7 = (f32[256]{0:T(256)S(1)}, f32[256]{0:T(256)}, u32[]{:S(2)}) copy-start(f32[256]{0:T(256)} %param.11) | copy-start | bytes 3076
